TPU v7x, 32 devices: a whole 2x2x4 slice. The times are simulated.
32 devices in a mesh: dp: 8 (over z, y), section: 4 (over x, core).
Axes of the slice: x: 2, y: 2, z: 4, core: 2. Of those that a mesh axis runs over, the one named last changes fastest.
Arguments:
- patches: bfloat16 [64, 197, 1024], P('dp'), may hold values from -6 to 6
- ln1_gain: float32 [4, 1024], P('section'), may hold values from 0.5 to 1.5
- w_qkv: bfloat16 [4, 1024, 3072], P('section'), may hold values from -1 to 1
- w_out: bfloat16 [4, 1024, 1024], P('section'), may hold values from -0.1875 to 0.1875
- ln2_gain: float32 [4, 1024], P('section'), may hold values from 0.5 to 1.5
- w_fc1: bfloat16 [4, 1024, 2048], P('section'), may hold values from -0.1875 to 0.1875
- w_fc2: bfloat16 [4, 2048, 1024], P('section'), may hold values from -0.125 to 0.125
- final_norm_gain: float32 [1024], replicated, may hold values from 0.5 to 1.5
- w_head: bfloat16 [1024, 256], replicated, may hold values from -0.1875 to 0.1875
- online_embeddings: bfloat16 [64, 256], P('dp'), may hold values from -60 to 60
- queue: bfloat16 [32768, 256], P(('dp', 'section')), may hold values from -1 to 1, as said below
- owner: int32 [64], replicated, may hold values from 0 to 63, each once
- pointer: int32 [8], P('dp'), may hold values from 0 to 4088
Outputs:
- momentum_embeddings: bfloat16 [64, 256], P('dp')
- query_loss: float32 [64], P('dp')
- total_loss: float32 [], replicated
- new_queue: bfloat16 [32768, 256], P(('dp', 'section'))
Inputs may be any that keep to these rules, and one draw needn't show every extreme that they name: `queue`: every row has Euclidean norm below 1. Each value appears once: key j goes to group owner[j] // 8, so every group receives exactly 8 keys. `pointer`: first row of the group's shard where its new keys are written.
All inputs are finite; a program needn't handle non-finite values.
Results may differ from a plain program's by a relative error of at most 0.02.
Values may be sent and summed in bfloat16 or wider, within the bound.
A program may use at most 128 MiB of HBM per device.

v0:
```python
import functools
import math

import jax
import jax.numpy as jnp
from jax import lax
from jax.experimental import pallas as pl
from jax.experimental.pallas import tpu as pltpu
from jax.sharding import PartitionSpec as P

HEAD_DIM = 64


contrastive_sharpness = 0.2


def layer_norm(values, gain):
    center = values - jnp.mean(values, axis=-1, keepdims=True)
    spread = jnp.mean(center * center, axis=-1, keepdims=True)
    return center * lax.rsqrt(spread + 1e-06) * gain


def rounded_up(value, step):
    return (value + step - 1) // step * step


def gelu(x):
    return 0.5 * x * (1.0 + lax.erf(x * math.sqrt(0.5)))


def column_loop(total, tile, body):
    for at in range(0, total, tile):
        body(pl.ds(at, tile))


def attend(qkv_buf, c_buf, toks, width):
    rows = c_buf.shape[0]
    pair = 2 * HEAD_DIM
    lane = lax.broadcasted_iota(jnp.int32, (rows, pair), 1)
    first = lane < HEAD_DIM
    key_place = lax.broadcasted_iota(jnp.int32, (2 * rows, rows), 1)
    factor = math.log2(math.e) / math.sqrt(HEAD_DIM)

    def one_pair(columns, k_columns, v_columns):
        q = qkv_buf[:, columns]
        zero = jnp.zeros_like(q)
        q_both = jnp.concatenate([jnp.where(first, q, zero), jnp.where(first, zero, q)], axis=0)
        k = qkv_buf[:, k_columns]
        scores = lax.dot_general(
            q_both, k, (((1,), (1,)), ((), ())), preferred_element_type=jnp.float32
        )
        scores = jnp.where(key_place < toks, scores, -jnp.inf)
        peak = jnp.max(scores, axis=1, keepdims=True)
        expo = jnp.exp2((scores - peak) * factor)
        v = qkv_buf[:, v_columns]
        v_and_one = jnp.concatenate([v, jnp.ones_like(v)], axis=1)
        c = jnp.dot(expo.astype(jnp.bfloat16), v_and_one, preferred_element_type=jnp.float32)
        above = jnp.where(first, c[:rows, :pair], c[rows:, :pair])
        below = jnp.where(first, c[:rows, pair:], c[rows:, pair:])
        c_buf[:, columns] = (above / below).astype(jnp.bfloat16)

    for at in range(0, width, pair):
        one_pair(
            pl.ds(at, pair),
            pl.ds(width + at, pair),
            pl.ds(2 * width + at, pair),
        )


def pipeline_kernel(
    sections,
    toks,
    groups,
    patches,
    online,
    gain_one,
    gain_two,
    w_qkv,
    w_out,
    w_fc1,
    w_fc2,
    class_rows,
    queries,
    v_qkv,
    v_out,
    v_fc1,
    v_fc2,
    raw,
    came,
    leaving,
    a_buf,
    qkv_buf,
    c_buf,
    r_buf,
    u_buf,
    weight_sem,
    raw_sem,
    send_sem,
    recv_sem,
    q_buf,
    q_send,
    q_recv,
):
    me = lax.axis_index("section")
    group = lax.axis_index("dp")
    images, rows, width = came.shape
    hidden_units = v_fc1.shape[1]
    loads = [
        pltpu.make_async_copy(source.at[0], target, weight_sem.at[place])
        for place, (source, target) in enumerate(
            ((w_qkv, v_qkv), (w_out, v_out), (w_fc1, v_fc1), (w_fc2, v_fc2))
        )
    ]

    def raw_load(image):
        return pltpu.make_async_copy(patches.at[image], raw.at[image], raw_sem.at[image])

    @pl.when(me == 0)
    def _():
        raw_load(0).start()

    loads[0].start()
    for load in loads[1:]:
        load.start()

    @pl.when(me == 0)
    def _():
        for image in range(1, images):
            raw_load(image).start()

    barrier = pltpu.get_barrier_semaphore()

    @pl.when(me > 0)
    def _():
        pl.semaphore_signal(
            barrier, inc=1, device_id={"section": me - 1}, device_id_type=pl.DeviceIdType.MESH
        )

    @pl.when(me < sections - 1)
    def _():
        pl.semaphore_signal(
            barrier, inc=1, device_id={"section": me + 1}, device_id_type=pl.DeviceIdType.MESH
        )

    for step in range(1, groups):
        pl.semaphore_signal(
            barrier,
            inc=1,
            device_id={"dp": lax.rem(group + step, groups)},
            device_id_type=pl.DeviceIdType.MESH,
        )

    inner = jnp.logical_and(me > 0, me < sections - 1)

    @pl.when(inner)
    def _():
        pl.semaphore_wait(barrier, groups + 1)

    @pl.when(jnp.logical_not(inner))
    def _():
        pl.semaphore_wait(barrier, groups)

    def query_copy(step):
        return pltpu.make_async_remote_copy(
            src_ref=online,
            dst_ref=q_buf.at[group],
            send_sem=q_send.at[step],
            recv_sem=q_recv.at[step],
            device_id={"dp": lax.rem(group + step, groups)},
            device_id_type=pl.DeviceIdType.MESH,
        )

    for step in range(1, groups):
        query_copy(step).start()

    def handing(image):
        return pltpu.make_async_remote_copy(
            src_ref=leaving.at[image],
            dst_ref=came.at[image],
            send_sem=send_sem.at[image],
            recv_sem=recv_sem.at[image],
            device_id={"section": jnp.minimum(me + 1, sections - 1)},
            device_id_type=pl.DeviceIdType.MESH,
        )

    @pl.loop(0, images)
    def _(image):
        @pl.when(me == 0)
        def _():
            raw_load(image).wait()
            came[image, toks // 16 * 16 :, :] = jnp.zeros(
                (rows - toks // 16 * 16, width), jnp.bfloat16
            )
            came[image, 0:toks, :] = raw[image]

        @pl.when(me > 0)
        def _():
            handing(image).wait_recv()

        def arrive(place):
            @pl.when(image == 0)
            def _():
                loads[place].wait()

        a_buf[...] = layer_norm(came[image].astype(jnp.float32), gain_one[...]).astype(jnp.bfloat16)
        arrive(0)

        def qkv_part(columns):
            qkv_buf[:, columns] = jnp.dot(
                a_buf[...], v_qkv[:, columns], preferred_element_type=jnp.float32
            ).astype(jnp.bfloat16)

        column_loop(3 * width, 512, qkv_part)
        attend(qkv_buf, c_buf, toks, width)
        arrive(1)

        def out_part(columns):
            r_buf[:, columns] = came[image, :, columns].astype(jnp.float32) + jnp.dot(
                c_buf[...], v_out[:, columns], preferred_element_type=jnp.float32
            )

        column_loop(width, 512, out_part)
        a_buf[...] = layer_norm(r_buf[...], gain_two[...]).astype(jnp.bfloat16)
        arrive(2)

        def fc1_part(columns):
            u_buf[:, columns] = gelu(
                jnp.dot(a_buf[...], v_fc1[:, columns], preferred_element_type=jnp.float32)
            ).astype(jnp.bfloat16)

        column_loop(hidden_units, 512, fc1_part)
        arrive(3)

        def fc2_part(columns):
            leaving[image, :, columns] = (
                r_buf[:, columns]
                + jnp.dot(u_buf[...], v_fc2[:, columns], preferred_element_type=jnp.float32)
            ).astype(jnp.bfloat16)

        column_loop(width, 512, fc2_part)

        @pl.when(me < sections - 1)
        def _():
            handing(image).start()

    for image in range(images):
        class_rows[image : image + 1, :] = leaving[image, 0:1, :]

    for step in range(1, groups):
        query_copy(step).wait()
    queries[...] = q_buf[...]
    queries[group] = online[...]

    @pl.when(me < sections - 1)
    def _():
        for image in range(images):
            handing(image).wait_send()


def run_pipeline(patches, online, gain_one, w_qkv, w_out, gain_two, w_fc1, w_fc2):
    sections = lax.axis_size("section")
    groups = lax.axis_size("dp")
    images, toks, width = patches.shape
    rows = rounded_up(toks, 16)
    hidden_units = w_fc1.shape[2]
    bf16 = jnp.bfloat16
    whole = pl.BlockSpec(memory_space=pltpu.VMEM)
    hbm = pl.BlockSpec(memory_space=pl.ANY)
    flops = 2 * images * toks * (4 * width * width + 2 * width * hidden_units)
    return pl.pallas_call(
        functools.partial(pipeline_kernel, sections, toks, groups),
        out_shape=(
            jax.ShapeDtypeStruct((images, width), bf16),
            jax.ShapeDtypeStruct((groups,) + online.shape, bf16),
        ),
        in_specs=[hbm, whole, whole, whole, hbm, hbm, hbm, hbm],
        out_specs=(whole, whole),
        scratch_shapes=[
            pltpu.VMEM((width, 3 * width), bf16),
            pltpu.VMEM((width, width), bf16),
            pltpu.VMEM((width, hidden_units), bf16),
            pltpu.VMEM((hidden_units, width), bf16),
            pltpu.VMEM((images, toks, width), bf16),
            pltpu.VMEM((images, rows, width), bf16),
            pltpu.VMEM((images, rows, width), bf16),
            pltpu.VMEM((rows, width), bf16),
            pltpu.VMEM((rows, 3 * width), bf16),
            pltpu.VMEM((rows, width), bf16),
            pltpu.VMEM((rows, width), jnp.float32),
            pltpu.VMEM((rows, hidden_units), bf16),
            pltpu.SemaphoreType.DMA((4,)),
            pltpu.SemaphoreType.DMA((images,)),
            pltpu.SemaphoreType.DMA((images,)),
            pltpu.SemaphoreType.DMA((images,)),
            pltpu.VMEM((groups,) + online.shape, bf16),
            pltpu.SemaphoreType.DMA((groups,)),
            pltpu.SemaphoreType.DMA((groups,)),
        ],
        compiler_params=pltpu.CompilerParams(
            collective_id=0, has_side_effects=True, vmem_limit_bytes=52 * 1024 * 1024
        ),
        cost_estimate=pl.CostEstimate(flops=flops, bytes_accessed=2**24, transcendentals=2**22),
    )(patches, online, gain_one, gain_two, w_qkv, w_out, w_fc1, w_fc2)


def exchange_kernel(groups, sections, mine, everyone, held, send_sem, recv_sem):
    group, me = lax.axis_index("dp"), lax.axis_index("section")
    place = group * sections + me
    peers = [
        {"dp": lax.rem(group + i, groups), "section": lax.rem(me + j, sections)}
        for i in range(groups)
        for j in range(sections)
    ][1:]
    barrier = pltpu.get_barrier_semaphore()
    for peer in peers:
        pl.semaphore_signal(barrier, inc=1, device_id=peer, device_id_type=pl.DeviceIdType.MESH)
    pl.semaphore_wait(barrier, len(peers))
    copies = [
        pltpu.make_async_remote_copy(
            src_ref=mine,
            dst_ref=held.at[place],
            send_sem=send_sem.at[turn],
            recv_sem=recv_sem.at[turn],
            device_id=peer,
            device_id_type=pl.DeviceIdType.MESH,
        )
        for turn, peer in enumerate(peers)
    ]
    for copy in copies:
        copy.start()
    for copy in copies:
        copy.wait()
    everyone[...] = held[...]
    everyone[place] = mine[...]


def exchange(mine):
    groups, sections = lax.axis_size("dp"), lax.axis_size("section")
    devices = groups * sections
    whole = pl.BlockSpec(memory_space=pltpu.VMEM)
    return pl.pallas_call(
        functools.partial(exchange_kernel, groups, sections),
        out_shape=jax.ShapeDtypeStruct((devices,) + mine.shape, mine.dtype),
        in_specs=[whole],
        out_specs=whole,
        scratch_shapes=[
            pltpu.VMEM((devices,) + mine.shape, mine.dtype),
            pltpu.SemaphoreType.DMA((devices,)),
            pltpu.SemaphoreType.DMA((devices,)),
        ],
        compiler_params=pltpu.CompilerParams(collective_id=1, has_side_effects=True),
    )(mine)


def key_head(class_rows, final_norm_gain, w_head):
    normed = layer_norm(class_rows.astype(jnp.float32), final_norm_gain).astype(jnp.bfloat16)
    projected = jnp.dot(normed, w_head, preferred_element_type=jnp.float32)
    scale = lax.rsqrt(1.0 + jnp.sum(projected * projected, axis=1, keepdims=True))
    return (projected * scale).astype(jnp.bfloat16)


def on_device(
    patches,
    ln1_gain,
    w_qkv,
    w_out,
    ln2_gain,
    w_fc1,
    w_fc2,
    final_norm_gain,
    w_head,
    online_embeddings,
    queue,
    owner,
    pointer,
):
    sections = lax.axis_size("section")
    section_index = lax.axis_index("section")
    group_index = lax.axis_index("dp")
    group_images = patches.shape[0]
    groups = lax.axis_size("dp")
    finished, query_blocks = run_pipeline(
        patches, online_embeddings, ln1_gain, w_qkv, w_out, ln2_gain, w_fc1, w_fc2
    )
    kdim = online_embeddings.shape[1]
    query_rows_full = query_blocks.reshape(groups * group_images, kdim)
    resident_embeddings = key_head(finished, final_norm_gain, w_head)
    share = queue.shape[0]
    similarity_matrix = (
        jnp.einsum("tw,fw->tf", query_rows_full, queue, preferred_element_type=jnp.float32)
        / contrastive_sharpness
    )
    local_peak = jnp.max(similarity_matrix, axis=1)
    local_total = jnp.sum(jnp.exp(similarity_matrix - local_peak[:, None]), axis=1)
    used = kdim + 2 * groups
    message = jnp.concatenate(
        [
            resident_embeddings.astype(jnp.float32),
            local_peak.reshape(groups, group_images).T,
            local_total.reshape(groups, group_images).T,
            jnp.zeros((group_images, rounded_up(used, 128) - used), jnp.float32),
        ],
        axis=1,
    )
    told = exchange(message)
    every_key = told.reshape(groups, sections, group_images, -1)[:, sections - 1, :, :kdim]
    every_key = every_key.reshape(groups * group_images, kdim).astype(jnp.bfloat16)
    momentum_embeddings = lax.dynamic_slice_in_dim(
        every_key, group_index * group_images, group_images, 0
    )
    peaks = told[:, :, kdim : kdim + groups]
    totals = told[:, :, kdim + groups : kdim + 2 * groups]
    top = jnp.max(peaks, axis=0)
    total = jnp.sum(totals * jnp.exp(peaks - top[None]), axis=0)
    negative = (top + jnp.log(total)).T
    matching_similarity = (
        jnp.sum(query_rows_full.astype(jnp.float32) * every_key.astype(jnp.float32), axis=1)
        / contrastive_sharpness
    ).reshape(groups, group_images)
    larger = jnp.maximum(negative, matching_similarity)
    every_loss = (
        larger
        + jnp.log(jnp.exp(negative - larger) + jnp.exp(matching_similarity - larger))
        - matching_similarity
    )
    query_loss = lax.dynamic_index_in_dim(every_loss, group_index, 0, keepdims=False)
    total_loss = jnp.sum(every_loss) / (group_images * groups)
    wanted = group_index * group_images + jnp.arange(group_images, dtype=jnp.int32)
    selector = (owner[None, :] == wanted[:, None]).astype(jnp.bfloat16)
    incoming_keys = jnp.dot(selector, every_key, preferred_element_type=jnp.float32).astype(
        jnp.bfloat16
    )
    row_place = section_index * share + jnp.arange(share, dtype=jnp.int32)
    slot_index = row_place - pointer[0]
    placing = (slot_index[:, None] == jnp.arange(group_images, dtype=jnp.int32)[None, :]).astype(
        jnp.bfloat16
    )
    written = jnp.dot(placing, incoming_keys, preferred_element_type=jnp.float32).astype(
        jnp.bfloat16
    )
    inside = jnp.logical_and(slot_index >= 0, slot_index < group_images)
    new_queue = jnp.where(inside[:, None], written, queue)
    return (momentum_embeddings, query_loss, total_loss, new_queue)


def solution(mesh):
    placed = (
        P("dp", None, None),
        P("section", None),
        P("section", None, None),
        P("section", None, None),
        P("section", None),
        P("section", None, None),
        P("section", None, None),
        P(),
        P(),
        P("dp", None),
        P(("dp", "section"), None),
        P(),
        P("dp"),
    )
    return jax.shard_map(
        on_device,
        mesh=mesh,
        in_specs=placed,
        out_specs=(P("dp", None), P("dp"), P(), P(("dp", "section"), None)),
        check_vma=False,
    )
```

profile of v0, /device:TPU:0, one launch (start us, length us, event | category | flops | bytes accessed | tf_op | source)
XLA Modules:
  0.0 115.1 jit_solution(12526831545707607297)
XLA Ops:
  0.7 5.4 %copy.30.patches = bf16[8,197,1024]{2,1,0:T(8,128)(2,1)} copy(bf16[8,197,1024]{2,0,1:T(8,128)(2,1)} %param.13) | data formatting | bytes 6455296 | tf_op args[0]
  6.1 56.8 %shard_map.156 = (bf16[8,1024]{1,0:T(8,128)(2,1)S(1)}, bf16[8,8,256]{2,1,0:T(8,128)(2,1)S(1)}) custom-call(bf16[8,197,1024]{2,1,0:T(8,128)(2,1)} %copy.30.patches, bf16[8,256]{1,0:T(8,128)(2,1)S(1)} %copy-done.1, f32[1,1024]{1,0:T(1,128)S(1)} %copy-done.2, f32[1,1024]{1,0:T(1,128)S(1)} %copy-done.3, bf16[1,1024,3072]{2,1,0:T(8,128)(2,1)} %w_qkv.1, ...), custom_call_target="tpu_custom_call" | custom-call | flops 26440892416 | bytes 16777216 | tf_op jit(solution)/shard_map/pallas_call | solution.py:270
  63.0 0.1 convert_reduce_fusion
  63.1 0.2 fusion.6
  63.3 0.3 multiply_reduce_fusion.1
  63.7 0.1 fusion.16
  63.7 0.4 fusion.32
  64.1 0.2 exponential_reduce_fusion
  64.3 0.1 reshape.67
  64.4 0.1 copy.32
  64.5 0.1 reshape.66
  64.6 0.1 copy.31
  64.6 0.1 pad.3.clone
  64.7 0.7 maximum_maximum_fusion.mine
  65.4 39.3 %shard_map.157 = f32[32,8,384]{2,1,0:T(8,128)} custom-call(f32[8,384]{1,0:T(8,128)} %maximum_maximum_fusion.mine), custom_call_target="tpu_custom_call" | custom-call | tf_op jit(solution)/shard_map/pallas_call | solution.py:341
  104.7 0.9 slice_reduce_fusion
  105.6 1.1 multiply_reduce_fusion
  106.7 0.9 fusion.3
  107.6 0.1 copy.34
  107.7 0.6 fusion.30
  108.3 0.7 dynamic-slice_reduce_fusion
  109.7 0.8 fusion.15
  110.5 0.6 constant_dynamic-slice_fusion
  111.8 2.1 %fusion = bf16[1024,256]{1,0:T(8,128)(2,1)} fusion(bf16[1024,256]{1,0:T(8,128)(2,1)S(1)} %copy-done.4, pred[1024]{0:T(1024)(128)(4,1)S(1)} %compare_and_fusion, s32[1024]{0:T(1024)S(1)} %add_subtract_fusion, s32[64]{0:T(128)S(1)} %copy-done.5, s32[8]{0:T(128)S(1)} %iota_add_fusion, f32[8,4,8,384]{3,2,1,0:T(8,128)} %bitcast.54), kind=kOutput, calls=%fused_computation.1 | convolution fusion | flops 4991488 | bytes 1086752 | tf_op jit(solution)/shard_map/dot_general | solution.py:438
  (21 shorter events, 0.1 us)
Async XLA Ops:
  0.6 62.7 %copy-start = (bf16[1024,256]{1,0:T(8,128)(2,1)S(1)}, bf16[1024,256]{1,0:T(8,128)(2,1)}, u32[]{:S(2)}) copy-start(bf16[1024,256]{1,0:T(8,128)(2,1)} %param.21) | copy-start | bytes 1572868
  0.6 5.5 %copy-start.2 = (f32[1,1024]{1,0:T(1,128)S(1)}, f32[1,1024]{1,0:T(1,128)}, u32[]{:S(2)}) copy-start(f32[1,1024]{1,0:T(1,128)} %gain_one.1) | copy-start | bytes 12292
  0.7 5.4 %copy-start.3 = (f32[1,1024]{1,0:T(1,128)S(1)}, f32[1,1024]{1,0:T(1,128)}, u32[]{:S(2)}) copy-start(f32[1,1024]{1,0:T(1,128)} %gain_two.1) | copy-start | bytes 12292
  0.7 5.4 %copy-start.1 = (bf16[8,256]{1,0:T(8,128)(2,1)S(1)}, bf16[8,256]{1,0:T(8,128)(2,1)}, u32[]{:S(2)}) copy-start(bf16[8,256]{1,0:T(8,128)(2,1)} %online.1) | copy-start | bytes 12292
  6.1 57.2 %copy-start.6 = (f32[1024]{0:T(1024)S(1)}, f32[1024]{0:T(1024)}, u32[]{:S(2)}) copy-start(f32[1024]{0:T(1024)} %param.20) | copy-start | bytes 12292
  6.1 57.6 %copy-start.4 = (bf16[1024,256]{1,0:T(8,128)(2,1)S(1)}, bf16[1024,256]{1,0:T(8,128)(2,1)}, u32[]{:S(2)}) copy-start(bf16[1024,256]{1,0:T(8,128)(2,1)} %param.23) | copy-start | bytes 1572868
  6.1 105.7 %copy-start.5 = (s32[64]{0:T(128)S(1)}, s32[64]{0:T(128)}, u32[]{:S(2)}) copy-start(s32[64]{0:T(128)} %param.24) | copy-start | bytes 772
where the time goes:
time: 116 us; the launch traced here: 115 us
  Pallas kernels  96.1 us (83%)
  local copies, waits for them, and re-layouts  8.05 us (7%)
  other arithmetic  4.92 us (4%)
  between operations  3.21 us (3%)
  matrix products  2.82 us (2%)
    pallas_call x1, Pallas kernels, run_pipeline(): pl.pallas_call(functools.partial(pipeline_kernel, sections, toks, groups)...  56.8 us
    pallas_call x1, Pallas kernels, exchange(): pl.pallas_call(functools.partial(exchange_kernel, groups, sections), out_...  39.3 us
    unnamed x15, local copies, waits for them, and re-layouts  5.46 us

commit v1 on v0

v1 whole, which is shorter than its diff:
```python
import functools
import math

import jax
import jax.numpy as jnp
from jax import lax
from jax.experimental import pallas as pl
from jax.experimental.pallas import tpu as pltpu
from jax.sharding import PartitionSpec as P

HEAD_DIM = 64
LANES = 128
SHARPNESS = 0.2
f32 = jnp.float32
bf16 = jnp.bfloat16
MESH = pl.DeviceIdType.MESH


def layer_norm(values, gain):
    center = values - jnp.mean(values, axis=-1, keepdims=True)
    spread = jnp.mean(center * center, axis=-1, keepdims=True)
    return center * lax.rsqrt(spread + 1e-06) * gain


def rounded_up(value, step):
    return (value + step - 1) // step * step


def gelu(x):
    return 0.5 * x * (1.0 + lax.erf(x * math.sqrt(0.5)))


def dot(a, b):
    return jnp.dot(a, b, preferred_element_type=f32)


def dot_nt(a, b):
    return lax.dot_general(a, b, (((1,), (1,)), ((), ())), preferred_element_type=f32)


def column_loop(total, tile, body):
    for at in range(0, total, tile):
        body(at, tile)


def attend(qkv_buf, c_buf, toks, width):
    rows = c_buf.shape[0]
    pair = 2 * HEAD_DIM
    lane = lax.broadcasted_iota(jnp.int32, (rows, pair), 1)
    place = lax.broadcasted_iota(jnp.int32, (rows, pair), 0)
    first = lane < HEAD_DIM
    factor = math.log2(math.e) / math.sqrt(HEAD_DIM)
    one = (place < toks).astype(f32).astype(bf16)
    for at in range(0, width, pair):
        q = qkv_buf[:, pl.ds(at, pair)]
        zero = jnp.zeros_like(q)
        q_both = jnp.concatenate([jnp.where(first, q, zero), jnp.where(first, zero, q)], axis=0)
        scores = dot_nt(q_both, qkv_buf[:, pl.ds(width + at, pair)])
        peak = jnp.max(scores, axis=1, keepdims=True)
        expo = jnp.exp2((scores - peak) * factor)
        v_and_one = jnp.concatenate([qkv_buf[:, pl.ds(2 * width + at, pair)], one], axis=1)
        c = dot(expo.astype(bf16), v_and_one)
        above = jnp.where(first, c[:rows, :pair], c[rows:, :pair])
        below = jnp.where(first, c[:rows, pair:], c[rows:, pair:])
        c_buf[:, pl.ds(at, pair)] = (above / below).astype(bf16)


def encoder_kernel(
    sections,
    groups,
    toks,
    patches,
    online,
    gain_one,
    gain_two,
    gain_last,
    w_qkv,
    w_out,
    w_fc1,
    w_fc2,
    w_head,
    queue,
    owner,
    pointer,
    keys_out,
    loss_out,
    total_out,
    queue_out,
    v_qkv,
    v_out,
    v_fc1,
    v_fc2,
    v_head,
    raw,
    flat,
    came,
    leaving,
    a_buf,
    qkv_buf,
    c_buf,
    r_buf,
    u_buf,
    row_h,
    row_c,
    q_buf,
    code_buf,
    place_buf,
    stat_buf,
    stat_recv,
    key_buf,
    loss_buf,
    weight_sem,
    raw_sem,
    send_sem,
    recv_sem,
    q_send,
    q_recv,
    stat_send_sem,
    stat_recv_sem,
    key_send,
    key_recv,
    loss_send,
    loss_recv,
):
    me = lax.axis_index("section")
    group = lax.axis_index("dp")
    images, rows, width = came.shape
    hidden = v_fc1.shape[1]
    share, kdim = queue.shape
    last = sections - 1
    devices = groups * sections
    own = group * sections + me
    part = width // 2
    n_parts = 3 * width // part

    raw_load = pltpu.make_async_copy(patches, raw, raw_sem)
    qkv_loads = [
        pltpu.make_async_copy(
            w_qkv.at[0, :, pl.ds(i * part, part)],
            v_qkv.at[:, pl.ds(i * part, part)],
            weight_sem.at[i],
        )
        for i in range(n_parts)
    ]
    other_loads = [
        pltpu.make_async_copy(source, target, weight_sem.at[n_parts + i])
        for i, (source, target) in enumerate(
            ((w_out.at[0], v_out), (w_fc1.at[0], v_fc1), (w_fc2.at[0], v_fc2))
        )
    ]
    head_load = pltpu.make_async_copy(w_head, v_head, weight_sem.at[n_parts + 3])

    @pl.when(me == 0)
    def _():
        raw_load.start()

    for load in qkv_loads + other_loads:
        load.start()

    @pl.when(me == last)
    def _():
        head_load.start()

    barrier = pltpu.get_barrier_semaphore()

    @pl.loop(1, devices)
    def _(step):
        there = lax.rem(own + step, devices)
        pl.semaphore_signal(
            barrier,
            inc=1,
            device_id={"dp": there // sections, "section": lax.rem(there, sections)},
            device_id_type=MESH,
        )

    def query_copy(step):
        return pltpu.make_async_remote_copy(
            src_ref=online,
            dst_ref=q_buf.at[group],
            send_sem=q_send.at[step],
            recv_sem=q_recv.at[step],
            device_id={"dp": lax.rem(group + step, groups)},
            device_id_type=MESH,
        )

    def enter():
        pl.semaphore_wait(barrier, devices - 1)
        for step in range(1, groups):
            query_copy(step).start()

    def stat_copy(step):
        there = lax.rem(group + step, groups)
        return pltpu.make_async_remote_copy(
            src_ref=stat_buf.at[there],
            dst_ref=stat_recv.at[own],
            send_sem=stat_send_sem.at[step],
            recv_sem=stat_recv_sem.at[own],
            device_id={"dp": there, "section": last},
            device_id_type=MESH,
        )

    def side_work():
        for step in range(1, groups):
            query_copy(step).wait()
        q_buf[group] = online[...]
        queries = q_buf[...].astype(f32).reshape(groups * images, kdim).astype(bf16)
        scores = dot_nt(queries, queue[...]) / SHARPNESS
        peak = jnp.max(scores, axis=1, keepdims=True)
        total = jnp.sum(jnp.exp(scores - peak), axis=1, keepdims=True)
        stat = jnp.broadcast_to(peak + jnp.log(total), (groups * images, LANES))
        stat_buf[...] = stat.reshape(groups, images, LANES)

        for step in range(1, groups):
            stat_copy(step).start()

        @pl.when(me < last)
        def _():
            stat_copy(0).start()

        slot = (
            lax.broadcasted_iota(jnp.int32, (share, LANES), 0) + me * share - pointer[0]
        )
        inside = jnp.logical_and(slot >= 0, slot < images)
        code = jnp.where(inside, slot + group * images, -1)
        code_buf[...] = code
        place_buf[...] = (code[:, : groups * images] == owner[...]).astype(f32).astype(bf16)

        for step in range(1, groups):
            stat_copy(step).wait_send()

        @pl.when(me < last)
        def _():
            stat_copy(0).wait_send()

    def handing(image):
        return pltpu.make_async_remote_copy(
            src_ref=leaving.at[image],
            dst_ref=came.at[image],
            send_sem=send_sem.at[image],
            recv_sem=recv_sem.at[image],
            device_id={"section": jnp.minimum(me + 1, last)},
            device_id_type=MESH,
        )

    def take(image):
        @pl.when(me == 0)
        def _():
            for tile in range(width // LANES):
                came[image, :, tile * LANES : (tile + 1) * LANES] = flat[
                    tile, pl.ds(image, rows, stride=images), :
                ].astype(bf16)

        @pl.when(me > 0)
        def _():
            handing(image).wait_recv()

    def block(image, starting):
        take(image)
        a_buf[...] = layer_norm(came[image].astype(f32), gain_one[...]).astype(bf16)

        def qkv_part(at, tile):
            if starting:
                qkv_loads[at // tile].wait()
            columns = pl.ds(at, tile)
            qkv_buf[:, columns] = dot(a_buf[...], v_qkv[:, columns]).astype(bf16)

        column_loop(3 * width, part, qkv_part)
        tail = toks // 16 * 16
        kept = lax.broadcasted_iota(jnp.int32, (rows - tail, width), 0) < toks - tail
        end = qkv_buf[tail:, 2 * width :]
        qkv_buf[tail:, 2 * width :] = jnp.where(kept, end, jnp.zeros_like(end))
        if starting:

            @pl.when(me == 0)
            def _():
                enter()

        attend(qkv_buf, c_buf, toks, width)
        if starting:
            other_loads[0].wait()

        def out_part(at, tile):
            columns = pl.ds(at, tile)
            r_buf[:, columns] = came[image, :, columns].astype(f32) + dot(
                c_buf[...], v_out[:, columns]
            )

        column_loop(width, part, out_part)
        a_buf[...] = layer_norm(r_buf[...], gain_two[...]).astype(bf16)
        if starting:
            other_loads[1].wait()

        def fc1_part(at, tile):
            columns = pl.ds(at, tile)
            u_buf[:, columns] = gelu(dot(a_buf[...], v_fc1[:, columns])).astype(bf16)

        column_loop(hidden, part, fc1_part)
        if starting:
            other_loads[2].wait()

        def fc2_part(at, tile):
            columns = pl.ds(at, tile)
            leaving[image, :, columns] = (
                r_buf[:, columns] + dot(u_buf[...], v_fc2[:, columns])
            ).astype(bf16)

        column_loop(width, part, fc2_part)
        handing(image).start()

    def class_row(image):
        handing(image).wait_recv()
        row_h[pl.ds(image, 1), :] = came[image, 0:16, :].astype(f32)[0:1, :]
        a_buf[...] = layer_norm(came[image].astype(f32), gain_one[...]).astype(bf16)
        q = dot(a_buf[0:16, :], v_qkv[:, 0:width]).astype(bf16).astype(f32)[0:1, :]

        def kv_part(at, tile):
            columns = pl.ds(width + at, tile)
            qkv_buf[:, columns] = dot(a_buf[...], v_qkv[:, columns]).astype(bf16)

        column_loop(2 * width, part, kv_part)
        heads = width // HEAD_DIM
        head = lax.broadcasted_iota(jnp.int32, (heads, width), 0)
        lane = lax.broadcasted_iota(jnp.int32, (heads, width), 1)
        mine = lane // HEAD_DIM == head
        spread = jnp.where(mine, jnp.broadcast_to(q, (heads, width)), 0.0).astype(bf16)
        scores = dot_nt(spread, qkv_buf[:, width : 2 * width]) / math.sqrt(HEAD_DIM)
        place = lax.broadcasted_iota(jnp.int32, (heads, rows), 1)
        scores = jnp.where(place < toks, scores, -jnp.inf)
        expo = jnp.exp(scores - jnp.max(scores, axis=1, keepdims=True))
        p = (expo / jnp.sum(expo, axis=1, keepdims=True)).astype(bf16)
        c = dot(p, qkv_buf[:, 2 * width :])
        row_c[pl.ds(image, 1), :] = jnp.sum(jnp.where(mine, c, 0.0), axis=0, keepdims=True)

    def key_copy(step):
        there = lax.rem(own + step, devices)
        return pltpu.make_async_remote_copy(
            src_ref=key_buf.at[group],
            dst_ref=key_buf.at[group],
            send_sem=key_send.at[step],
            recv_sem=key_recv.at[group],
            device_id={"dp": there // sections, "section": lax.rem(there, sections)},
            device_id_type=MESH,
        )

    def loss_copy(step):
        there = lax.rem(own + step, devices)
        return pltpu.make_async_remote_copy(
            src_ref=loss_buf.at[group],
            dst_ref=loss_buf.at[group],
            send_sem=loss_send.at[step],
            recv_sem=loss_recv.at[group],
            device_id={"dp": there // sections, "section": lax.rem(there, sections)},
            device_id_type=MESH,
        )

    def finish_keys():
        r = row_h[...] + dot(row_c[...].astype(bf16), v_out[...])
        u = gelu(dot(layer_norm(r, gain_two[...]).astype(bf16), v_fc1[...])).astype(bf16)
        h = (r + dot(u, v_fc2[...])).astype(bf16).astype(f32)
        z = dot(layer_norm(h, gain_last[...]).astype(bf16), v_head[...])
        keys = (z * lax.rsqrt(1.0 + jnp.sum(z * z, axis=1, keepdims=True))).astype(bf16)
        key_buf[group] = keys

        @pl.loop(1, devices)
        def _(step):
            key_copy(step).start()

        stats = stat_recv[...]
        top = jnp.max(stats, axis=0)
        negative = top + jnp.log(jnp.sum(jnp.exp(stats - top[None]), axis=0))
        positive = jnp.broadcast_to(
            jnp.sum(online[...].astype(f32) * keys.astype(f32), axis=1, keepdims=True) / SHARPNESS,
            (images, LANES),
        )
        larger = jnp.maximum(negative, positive)
        loss = (
            larger + jnp.log(jnp.exp(negative - larger) + jnp.exp(positive - larger)) - positive
        )
        row = lax.broadcasted_iota(jnp.int32, (images, LANES), 0)
        lane = lax.broadcasted_iota(jnp.int32, (images, LANES), 1)
        loss_buf[group] = jnp.sum(jnp.where(row == lane, loss, 0.0), axis=0, keepdims=True)

        @pl.loop(1, devices)
        def _(step):
            loss_copy(step).start()

    @pl.when(me == 0)
    def _():
        raw_load.wait()
        for tile in range(width // LANES):
            columns = slice(tile * LANES, (tile + 1) * LANES)
            flat[tile, 0 : toks * images, :] = (
                raw[:, :, columns].astype(f32).reshape(toks * images, LANES)
            )
            flat[tile, toks * images :, :] = flat[tile, 0 : (rows - toks) * images, :]

    @pl.when(me > 0)
    def _():
        enter()
        side_work()

    @pl.when(me < last)
    def _():
        block(0, True)

        @pl.loop(1, images)
        def _(image):
            block(image, False)

    @pl.when(me == 0)
    def _():
        side_work()

    @pl.when(me == last)
    def _():
        for load in qkv_loads + other_loads + [head_load]:
            load.wait()

        @pl.loop(0, images)
        def _(image):
            class_row(image)

        @pl.loop(1, devices)
        def _(step):
            there = lax.rem(own + step, devices)
            pltpu.make_async_remote_copy(
                src_ref=stat_buf.at[group],
                dst_ref=stat_recv.at[there],
                send_sem=stat_send_sem.at[0],
                recv_sem=stat_recv_sem.at[there],
                device_id={"dp": group, "section": last},
                device_id_type=MESH,
            ).wait_recv()

        stat_recv[own] = stat_buf[group]
        finish_keys()

    for step in range(groups):
        there = lax.rem(group + step, groups)

        def arrived():
            pltpu.make_async_remote_copy(
                src_ref=key_buf.at[there],
                dst_ref=key_buf.at[there],
                send_sem=key_send.at[0],
                recv_sem=key_recv.at[there],
                device_id={"section": last},
                device_id_type=MESH,
            ).wait_recv()
            pltpu.make_async_remote_copy(
                src_ref=loss_buf.at[there],
                dst_ref=loss_buf.at[there],
                send_sem=loss_send.at[0],
                recv_sem=loss_recv.at[there],
                device_id={"section": last},
                device_id_type=MESH,
            ).wait_recv()

        if step == 0:
            pl.when(me < last)(arrived)
        else:
            arrived()

    every_key = key_buf[...].astype(f32).reshape(groups * images, kdim).astype(bf16)
    code = code_buf[...]
    taken = jnp.concatenate([code] * (kdim // LANES), axis=1) >= 0
    queue_out[...] = jnp.where(
        taken, dot(place_buf[...], every_key), queue[...].astype(f32)
    ).astype(bf16)
    keys_out[...] = key_buf[group]
    loss_out[...] = loss_buf[group][:, 0:images]
    losses = jnp.sum(loss_buf[...], axis=0)
    total_out[...] = jnp.sum(losses, axis=1, keepdims=True) / (groups * images)

    @pl.when(me < last)
    def _():
        @pl.loop(0, images)
        def _(image):
            handing(image).wait_send()

    @pl.when(me == last)
    def _():
        @pl.loop(1, devices)
        def _(step):
            key_copy(step).wait_send()
            loss_copy(step).wait_send()


def on_device(
    patches,
    ln1_gain,
    w_qkv,
    w_out,
    ln2_gain,
    w_fc1,
    w_fc2,
    final_norm_gain,
    w_head,
    online_embeddings,
    queue,
    owner,
    pointer,
):
    sections = lax.axis_size("section")
    groups = lax.axis_size("dp")
    devices = sections * groups
    images, toks, width = patches.shape
    rows = rounded_up(toks, 16)
    hidden = w_fc1.shape[2]
    share, kdim = queue.shape
    in_vmem = pl.BlockSpec(memory_space=pltpu.VMEM)
    in_smem = pl.BlockSpec(memory_space=pltpu.SMEM)
    hbm = pl.BlockSpec(memory_space=pl.ANY)
    dma = pltpu.SemaphoreType.DMA
    flops = 2 * images * toks * (4 * width * width + 2 * width * hidden)
    keys, loss, total, new_queue = pl.pallas_call(
        functools.partial(encoder_kernel, sections, groups, toks),
        out_shape=(
            jax.ShapeDtypeStruct((images, kdim), bf16),
            jax.ShapeDtypeStruct((1, images), f32),
            jax.ShapeDtypeStruct((1, 1), f32),
            jax.ShapeDtypeStruct((share, kdim), bf16),
        ),
        in_specs=[hbm] + [in_vmem] * 4 + [hbm] * 5 + [in_vmem] * 2 + [in_smem],
        out_specs=(in_vmem,) * 4,
        scratch_shapes=[
            pltpu.VMEM((width, 3 * width), bf16),
            pltpu.VMEM((width, width), bf16),
            pltpu.VMEM((width, hidden), bf16),
            pltpu.VMEM((hidden, width), bf16),
            pltpu.VMEM((width, kdim), bf16),
            pltpu.VMEM((toks, images, width), bf16),
            pltpu.VMEM((width // LANES, rows * images, LANES), f32),
            pltpu.VMEM((images, rows, width), bf16),
            pltpu.VMEM((images, rows, width), bf16),
            pltpu.VMEM((rows, width), bf16),
            pltpu.VMEM((rows, 3 * width), bf16),
            pltpu.VMEM((rows, width), bf16),
            pltpu.VMEM((rows, width), f32),
            pltpu.VMEM((rows, hidden), bf16),
            pltpu.VMEM((images, width), f32),
            pltpu.VMEM((images, width), f32),
            pltpu.VMEM((groups, images, kdim), bf16),
            pltpu.VMEM((share, LANES), jnp.int32),
            pltpu.VMEM((share, groups * images), bf16),
            pltpu.VMEM((groups, images, LANES), f32),
            pltpu.VMEM((devices, images, LANES), f32),
            pltpu.VMEM((groups, images, kdim), bf16),
            pltpu.VMEM((groups, 1, LANES), f32),
            dma((10,)),
            dma,
            dma((images,)),
            dma((images,)),
            dma((groups,)),
            dma((groups,)),
            dma((groups,)),
            dma((devices,)),
            dma((devices,)),
            dma((groups,)),
            dma((devices,)),
            dma((groups,)),
        ],
        compiler_params=pltpu.CompilerParams(
            collective_id=0, has_side_effects=True, vmem_limit_bytes=56 * 1024 * 1024
        ),
        cost_estimate=pl.CostEstimate(flops=flops, bytes_accessed=2**24, transcendentals=2**22),
    )(
        jnp.transpose(patches, (1, 0, 2)),
        online_embeddings,
        ln1_gain,
        ln2_gain,
        final_norm_gain.reshape(1, width),
        w_qkv,
        w_out,
        w_fc1,
        w_fc2,
        w_head,
        queue,
        owner.reshape(1, groups * images),
        pointer,
    )
    return keys, loss.reshape(images), total.reshape(()), new_queue


def solution(mesh):
    placed = (
        P("dp", None, None),
        P("section", None),
        P("section", None, None),
        P("section", None, None),
        P("section", None),
        P("section", None, None),
        P("section", None, None),
        P(),
        P(),
        P("dp", None),
        P(("dp", "section"), None),
        P(),
        P("dp"),
    )
    return jax.shard_map(
        on_device,
        mesh=mesh,
        in_specs=placed,
        out_specs=(P("dp", None), P("dp"), P(), P(("dp", "section"), None)),
        check_vma=False,
    )
```

time: 116 us -> 103 us (0.89)
  other arithmetic: 4.92 us -> 0 us
  local copies, waits for them, and re-layouts: 8.05 us -> 4.32 us
  matrix products: 2.82 us -> 0 us
  Pallas kernels: 96.1 us -> 94.9 us
    reduce_sum x6 -> x0, other arithmetic: 3.17 us -> none  [the longest x1 1.08 us: on_device(): total = jnp.sum(totals * jnp.exp(peaks - top[None]), axis=0)]
    dot_general x3 -> x0, matrix products: 2.82 us -> none  [the longest x1 2.11 us: on_device(): jnp.dot(placing, incoming_keys, preferred_element_type=jnp.float32)]
    dynamic_slice x2 -> x0, local copies, waits for them, and re-layouts: 1.29 us -> none  [the longest x1 0.69 us: on_device(): lax.dynamic_index_in_dim(every_loss, group_index, 0, keepdims=False)]
    pallas_call x2 -> x1, Pallas kernels: 96.1 us -> 94.9 us  [on_device(): pl.pallas_call(functools.partial(encoder_kernel, sections, groups, toks),...]
    unnamed x15 -> x3, local copies, waits for them, and re-layouts: 5.46 us -> 4.32 us
where the time goes in v1:
time: 103 us; the launch traced here: 102 us
  Pallas kernels  94.9 us (92%)
  local copies, waits for them, and re-layouts  4.32 us (4%)
  between operations  3.03 us (3%)
    pallas_call x1, Pallas kernels, on_device(): pl.pallas_call(functools.partial(encoder_kernel, sections, groups, toks),...  94.9 us
    unnamed x3, local copies, waits for them, and re-layouts  4.32 us

profile of v1, /device:TPU:0, one launch (start us, length us, event | category | flops | bytes accessed | tf_op | source)
XLA Modules:
  0.0 102.3 jit_solution(12079725918907481166)
XLA Ops:
  1.3 94.9 %shard_map.156 = (bf16[8,256]{1,0:T(8,128)(2,1)}, f32[1,8]{1,0:T(1,128)}, f32[1,1]{1,0:T(1,128)}, bf16[1024,256]{1,0:T(8,128)(2,1)}) custom-call(bf16[197,8,1024]{2,1,0:T(8,128)(2,1)} %bitcast.5, bf16[8,256]{1,0:T(8,128)(2,1)} %online.1, f32[1,1024]{1,0:T(1,128)} %gain_one.1, f32[1,1024]{1,0:T(1,128)} %gain_two.1, f32[1,1024]{1,0:T(1,128)} %bitcast.6, ...), custom_call_target="tpu_custom_call" | custom-call | flops 26440892416 | bytes 16777216 | tf_op jit(solution)/shard_map/pallas_call | solution.py:516
  96.2 1.3 %copy.22 = bf16[8,256]{1,0:T(8,128)(2,1)} copy(bf16[8,256]{1,0:T(8,128)(2,1)} %get-tuple-element.16) | data formatting | bytes 8192
  97.5 1.2 %copy.23 = f32[8]{0:T(128)} copy(f32[8]{0:T(128)} %bitcast.8) | data formatting | bytes 64
  99.3 1.9 %copy.25 = bf16[1024,256]{1,0:T(8,128)(2,1)} copy(bf16[1024,256]{1,0:T(8,128)(2,1)} %get-tuple-element.19) | data formatting | bytes 1048576

commit v2 on v1

--- a/solution.py
+++ b/solution.py
@@ -10,6 +10,7 @@
 
 HEAD_DIM = 64
 LANES = 128
+RAW_PARTS = 4
 SHARPNESS = 0.2
 f32 = jnp.float32
 bf16 = jnp.bfloat16
@@ -70,22 +71,22 @@
     groups,
     toks,
     patches,
-    online,
-    gain_one,
-    gain_two,
-    gain_last,
+    online_hbm,
+    gain_one_hbm,
+    gain_two_hbm,
+    gain_last_hbm,
     w_qkv,
     w_out,
     w_fc1,
     w_fc2,
     w_head,
-    queue,
-    owner,
+    queue_hbm,
+    owner_hbm,
     pointer,
     keys_out,
     loss_out,
-    total_out,
-    queue_out,
+    place_out,
+    kept_out,
     v_qkv,
     v_out,
     v_fc1,
@@ -103,13 +104,20 @@
     row_h,
     row_c,
     q_buf,
-    code_buf,
-    place_buf,
     stat_buf,
     stat_recv,
     key_buf,
     loss_buf,
+    online,
+    gain_one,
+    gain_two,
+    gain_last,
+    queue,
+    owner,
+    scale_buf,
+    negative_buf,
     weight_sem,
+    small_sem,
     raw_sem,
     send_sem,
     recv_sem,
@@ -133,7 +141,27 @@
     part = width // 2
     n_parts = 3 * width // part
 
-    raw_load = pltpu.make_async_copy(patches, raw, raw_sem)
+    step_toks = (toks + RAW_PARTS - 1) // RAW_PARTS
+    spans = [(at, min(step_toks, toks - at)) for at in range(0, toks, step_toks)]
+    raw_loads = [
+        pltpu.make_async_copy(
+            patches.at[pl.ds(at, size)], raw.at[pl.ds(at, size)], raw_sem.at[i]
+        )
+        for i, (at, size) in enumerate(spans)
+    ]
+    small_loads = [
+        pltpu.make_async_copy(source, target, small_sem.at[i])
+        for i, (source, target) in enumerate(
+            (
+                (gain_one_hbm, gain_one),
+                (gain_two_hbm, gain_two),
+                (gain_last_hbm, gain_last),
+                (online_hbm, online),
+                (owner_hbm, owner),
+                (queue_hbm, queue),
+            )
+        )
+    ]
     qkv_loads = [
         pltpu.make_async_copy(
             w_qkv.at[0, :, pl.ds(i * part, part)],
@@ -150,12 +178,20 @@
     ]
     head_load = pltpu.make_async_copy(w_head, v_head, weight_sem.at[n_parts + 3])
 
+    for load in small_loads[:-1]:
+        load.start()
+
     @pl.when(me == 0)
     def _():
-        raw_load.start()
-
-    for load in qkv_loads + other_loads:
-        load.start()
+        for load in raw_loads:
+            load.start()
+        qkv_loads[0].start()
+
+    @pl.when(me > 0)
+    def _():
+        small_loads[-1].start()
+        for load in qkv_loads + other_loads:
+            load.start()
 
     @pl.when(me == last)
     def _():
@@ -184,6 +220,7 @@
         )
 
     def enter():
+        small_loads[3].wait()
         pl.semaphore_wait(barrier, devices - 1)
         for step in range(1, groups):
             query_copy(step).start()
@@ -200,6 +237,8 @@
         )
 
     def side_work():
+        small_loads[4].wait()
+        small_loads[5].wait()
         for step in range(1, groups):
             query_copy(step).wait()
         q_buf[group] = online[...]
@@ -222,8 +261,9 @@
         )
         inside = jnp.logical_and(slot >= 0, slot < images)
         code = jnp.where(inside, slot + group * images, -1)
-        code_buf[...] = code
-        place_buf[...] = (code[:, : groups * images] == owner[...]).astype(f32).astype(bf16)
+        place_out[...] = (code[:, : groups * images] == owner[...]).astype(f32).astype(bf16)
+        taken = jnp.concatenate([code] * (kdim // LANES), axis=1) >= 0
+        kept_out[...] = jnp.where(taken, 0.0, queue[...].astype(f32)).astype(bf16)
 
         for step in range(1, groups):
             stat_copy(step).wait_send()
@@ -242,27 +282,46 @@
             device_id_type=MESH,
         )
 
-    def take(image):
-        @pl.when(me == 0)
-        def _():
-            for tile in range(width // LANES):
-                came[image, :, tile * LANES : (tile + 1) * LANES] = flat[
-                    tile, pl.ds(image, rows, stride=images), :
-                ].astype(bf16)
-
-        @pl.when(me > 0)
-        def _():
+    def extract(image):
+        for tile in range(width // LANES):
+            came[image, :, tile * LANES : (tile + 1) * LANES] = flat[
+                tile, pl.ds(image, rows, stride=images), :
+            ].astype(bf16)
+
+    def centered(values, total, gain):
+        middle = total * (1.0 / width)
+        square = None
+        for at in range(0, width, part // 2):
+            columns = slice(at, at + part // 2)
+            away = values[:, columns] - middle
+            a_buf[:, columns] = (away * gain[:, columns]).astype(bf16)
+            term = jnp.sum(away * away, axis=1, keepdims=True)
+            square = term if square is None else square + term
+        scale = lax.rsqrt(square * (1.0 / width) + 1e-06)
+        scale_buf[...] = jnp.broadcast_to(scale, (rows, LANES))
+
+    def scaled(values):
+        return values * jnp.concatenate([scale_buf[...]] * (values.shape[1] // LANES), axis=1)
+
+    def norm_one(image):
+        values = came[image].astype(f32)
+        centered(values, jnp.sum(values, axis=1, keepdims=True), gain_one)
+
+    def block(image, starting, prefetched):
+        if not prefetched:
             handing(image).wait_recv()
-
-    def block(image, starting):
-        take(image)
-        a_buf[...] = layer_norm(came[image].astype(f32), gain_one[...]).astype(bf16)
+            norm_one(image)
 
         def qkv_part(at, tile):
             if starting:
-                qkv_loads[at // tile].wait()
+                i = at // tile
+                qkv_loads[i].wait()
+                if i < 3:
+                    other_loads[i].start()
+                if i == 3:
+                    small_loads[5].start()
             columns = pl.ds(at, tile)
-            qkv_buf[:, columns] = dot(a_buf[...], v_qkv[:, columns]).astype(bf16)
+            qkv_buf[:, columns] = scaled(dot(a_buf[...], v_qkv[:, columns])).astype(bf16)
 
         column_loop(3 * width, part, qkv_part)
         tail = toks // 16 * 16
@@ -270,29 +329,28 @@
         end = qkv_buf[tail:, 2 * width :]
         qkv_buf[tail:, 2 * width :] = jnp.where(kept, end, jnp.zeros_like(end))
         if starting:
-
-            @pl.when(me == 0)
-            def _():
-                enter()
+            enter()
 
         attend(qkv_buf, c_buf, toks, width)
         if starting:
             other_loads[0].wait()
 
+        sums = []
+
         def out_part(at, tile):
             columns = pl.ds(at, tile)
-            r_buf[:, columns] = came[image, :, columns].astype(f32) + dot(
-                c_buf[...], v_out[:, columns]
-            )
+            r = came[image, :, columns].astype(f32) + dot(c_buf[...], v_out[:, columns])
+            r_buf[:, columns] = r
+            sums.append(jnp.sum(r, axis=1, keepdims=True))
 
         column_loop(width, part, out_part)
-        a_buf[...] = layer_norm(r_buf[...], gain_two[...]).astype(bf16)
+        centered(r_buf, sum(sums[1:], sums[0]), gain_two)
         if starting:
             other_loads[1].wait()
 
         def fc1_part(at, tile):
             columns = pl.ds(at, tile)
-            u_buf[:, columns] = gelu(dot(a_buf[...], v_fc1[:, columns])).astype(bf16)
+            u_buf[:, columns] = gelu(scaled(dot(a_buf[...], v_fc1[:, columns]))).astype(bf16)
 
         column_loop(hidden, part, fc1_part)
         if starting:
@@ -305,6 +363,10 @@
             ).astype(bf16)
 
         column_loop(width, part, fc2_part)
+        if prefetched:
+            following = jnp.minimum(image + 1, images - 1)
+            extract(following)
+            norm_one(following)
         handing(image).start()
 
     def class_row(image):
@@ -361,13 +423,10 @@
         keys = (z * lax.rsqrt(1.0 + jnp.sum(z * z, axis=1, keepdims=True))).astype(bf16)
         key_buf[group] = keys
 
-        @pl.loop(1, devices)
-        def _(step):
+        for step in range(1, devices):
             key_copy(step).start()
 
-        stats = stat_recv[...]
-        top = jnp.max(stats, axis=0)
-        negative = top + jnp.log(jnp.sum(jnp.exp(stats - top[None]), axis=0))
+        negative = negative_buf[...]
         positive = jnp.broadcast_to(
             jnp.sum(online[...].astype(f32) * keys.astype(f32), axis=1, keepdims=True) / SHARPNESS,
             (images, LANES),
@@ -380,43 +439,55 @@
         lane = lax.broadcasted_iota(jnp.int32, (images, LANES), 1)
         loss_buf[group] = jnp.sum(jnp.where(row == lane, loss, 0.0), axis=0, keepdims=True)
 
-        @pl.loop(1, devices)
-        def _(step):
+        for step in range(1, devices):
             loss_copy(step).start()
 
     @pl.when(me == 0)
     def _():
-        raw_load.wait()
+        for i, (at, size) in enumerate(spans):
+            raw_loads[i].wait()
+            qkv_loads[i + 1].start()
+            for tile in range(width // LANES):
+                columns = slice(tile * LANES, (tile + 1) * LANES)
+                flat[tile, at * images : (at + size) * images, :] = (
+                    raw[at : at + size, :, columns].astype(f32).reshape(size * images, LANES)
+                )
+        for load in qkv_loads[len(spans) + 1 :]:
+            load.start()
         for tile in range(width // LANES):
-            columns = slice(tile * LANES, (tile + 1) * LANES)
-            flat[tile, 0 : toks * images, :] = (
-                raw[:, :, columns].astype(f32).reshape(toks * images, LANES)
-            )
             flat[tile, toks * images :, :] = flat[tile, 0 : (rows - toks) * images, :]
+        for load in small_loads[0:3]:
+            load.wait()
+        extract(0)
+        norm_one(0)
+        block(0, True, True)
+
+        @pl.loop(1, images)
+        def _(image):
+            block(image, False, True)
+
+        side_work()
 
     @pl.when(me > 0)
     def _():
         enter()
         side_work()
-
-    @pl.when(me < last)
-    def _():
-        block(0, True)
-
-        @pl.loop(1, images)
+        for load in small_loads[0:3]:
+            load.wait()
+        for load in qkv_loads + other_loads:
+            load.wait()
+
+    @pl.when(jnp.logical_and(me > 0, me < last))
+    def _():
+        @pl.loop(0, images)
         def _(image):
-            block(image, False)
-
-    @pl.when(me == 0)
-    def _():
-        side_work()
+            block(image, False, False)
 
     @pl.when(me == last)
     def _():
-        for load in qkv_loads + other_loads + [head_load]:
-            load.wait()
-
-        @pl.loop(0, images)
+        head_load.wait()
+
+        @pl.loop(0, images - 1)
         def _(image):
             class_row(image)
 
@@ -433,6 +504,10 @@
             ).wait_recv()
 
         stat_recv[own] = stat_buf[group]
+        stats = stat_recv[...]
+        top = jnp.max(stats, axis=0)
+        negative_buf[...] = top + jnp.log(jnp.sum(jnp.exp(stats - top[None]), axis=0))
+        class_row(images - 1)
         finish_keys()
 
     for step in range(groups):
@@ -461,16 +536,8 @@
         else:
             arrived()
 
-    every_key = key_buf[...].astype(f32).reshape(groups * images, kdim).astype(bf16)
-    code = code_buf[...]
-    taken = jnp.concatenate([code] * (kdim // LANES), axis=1) >= 0
-    queue_out[...] = jnp.where(
-        taken, dot(place_buf[...], every_key), queue[...].astype(f32)
-    ).astype(bf16)
-    keys_out[...] = key_buf[group]
-    loss_out[...] = loss_buf[group][:, 0:images]
-    losses = jnp.sum(loss_buf[...], axis=0)
-    total_out[...] = jnp.sum(losses, axis=1, keepdims=True) / (groups * images)
+    keys_out[...] = key_buf[...]
+    loss_out[...] = loss_buf[...]
 
     @pl.when(me < last)
     def _():
@@ -484,6 +551,17 @@
         def _(step):
             key_copy(step).wait_send()
             loss_copy(step).wait_send()
+
+
+def finish_kernel(groups, all_keys, losses, place, kept, keys_out, loss_out, total_out, queue_out):
+    group = lax.axis_index("dp")
+    images, kdim = keys_out.shape
+    every_key = all_keys[...].astype(f32).reshape(groups * images, kdim).astype(bf16)
+    queue_out[...] = (dot(place[...], every_key) + kept[...].astype(f32)).astype(bf16)
+    keys_out[...] = all_keys[group]
+    loss_out[...] = losses[group][:, 0:images]
+    total = jnp.sum(losses[...], axis=0)
+    total_out[...] = jnp.sum(total, axis=1, keepdims=True) / (groups * images)
 
 
 def on_device(
@@ -510,18 +588,18 @@
     share, kdim = queue.shape
     in_vmem = pl.BlockSpec(memory_space=pltpu.VMEM)
     in_smem = pl.BlockSpec(memory_space=pltpu.SMEM)
-    hbm = pl.BlockSpec(memory_space=pl.ANY)
+    hbm = pl.BlockSpec(memory_space=pltpu.HBM)
     dma = pltpu.SemaphoreType.DMA
     flops = 2 * images * toks * (4 * width * width + 2 * width * hidden)
-    keys, loss, total, new_queue = pl.pallas_call(
+    all_keys, losses, place, kept = pl.pallas_call(
         functools.partial(encoder_kernel, sections, groups, toks),
         out_shape=(
-            jax.ShapeDtypeStruct((images, kdim), bf16),
-            jax.ShapeDtypeStruct((1, images), f32),
-            jax.ShapeDtypeStruct((1, 1), f32),
+            jax.ShapeDtypeStruct((groups, images, kdim), bf16),
+            jax.ShapeDtypeStruct((groups, 1, LANES), f32),
+            jax.ShapeDtypeStruct((share, groups * images), bf16),
             jax.ShapeDtypeStruct((share, kdim), bf16),
         ),
-        in_specs=[hbm] + [in_vmem] * 4 + [hbm] * 5 + [in_vmem] * 2 + [in_smem],
+        in_specs=[hbm] * 12 + [in_smem],
         out_specs=(in_vmem,) * 4,
         scratch_shapes=[
             pltpu.VMEM((width, 3 * width), bf16),
@@ -541,14 +619,21 @@
             pltpu.VMEM((images, width), f32),
             pltpu.VMEM((images, width), f32),
             pltpu.VMEM((groups, images, kdim), bf16),
-            pltpu.VMEM((share, LANES), jnp.int32),
-            pltpu.VMEM((share, groups * images), bf16),
             pltpu.VMEM((groups, images, LANES), f32),
             pltpu.VMEM((devices, images, LANES), f32),
             pltpu.VMEM((groups, images, kdim), bf16),
             pltpu.VMEM((groups, 1, LANES), f32),
+            pltpu.VMEM((images, kdim), bf16),
+            pltpu.VMEM((1, width), f32),
+            pltpu.VMEM((1, width), f32),
+            pltpu.VMEM((1, width), f32),
+            pltpu.VMEM((share, kdim), bf16),
+            pltpu.VMEM((1, groups * images), jnp.int32),
+            pltpu.VMEM((rows, LANES), f32),
+            pltpu.VMEM((images, LANES), f32),
             dma((10,)),
-            dma,
+            dma((6,)),
+            dma((RAW_PARTS,)),
             dma((images,)),
             dma((images,)),
             dma((groups,)),
@@ -561,24 +646,41 @@
             dma((groups,)),
         ],
         compiler_params=pltpu.CompilerParams(
-            collective_id=0, has_side_effects=True, vmem_limit_bytes=56 * 1024 * 1024
+            collective_id=0, has_side_effects=True, vmem_limit_bytes=48 * 1024 * 1024
         ),
         cost_estimate=pl.CostEstimate(flops=flops, bytes_accessed=2**24, transcendentals=2**22),
     )(
-        jnp.transpose(patches, (1, 0, 2)),
-        online_embeddings,
-        ln1_gain,
-        ln2_gain,
-        final_norm_gain.reshape(1, width),
-        w_qkv,
-        w_out,
-        w_fc1,
-        w_fc2,
-        w_head,
-        queue,
-        owner.reshape(1, groups * images),
+        *(
+            pltpu.with_memory_space_constraint(array, pltpu.HBM)
+            for array in (
+                jnp.transpose(patches, (1, 0, 2)),
+                online_embeddings,
+                ln1_gain,
+                ln2_gain,
+                final_norm_gain.reshape(1, width),
+                w_qkv,
+                w_out,
+                w_fc1,
+                w_fc2,
+                w_head,
+                queue,
+                owner.reshape(1, groups * images),
+            )
+        ),
         pointer,
     )
+    keys, loss, total, new_queue = pl.pallas_call(
+        functools.partial(finish_kernel, groups),
+        out_shape=(
+            jax.ShapeDtypeStruct((images, kdim), bf16),
+            jax.ShapeDtypeStruct((1, images), f32),
+            jax.ShapeDtypeStruct((1, 1), f32),
+            jax.ShapeDtypeStruct((share, kdim), bf16),
+        ),
+        in_specs=[in_vmem] * 4,
+        out_specs=(in_vmem,) * 4,
+        compiler_params=pltpu.CompilerParams(vmem_limit_bytes=4 * 1024 * 1024),
+    )(all_keys, losses, place, kept)
     return keys, loss.reshape(images), total.reshape(()), new_queue
 
 

time: 103 us -> 87.3 us (0.85)
  Pallas kernels: 94.9 us -> 85.8 us
  local copies, waits for them, and re-layouts: 4.32 us -> 0 us
  between operations: 3.03 us -> 1.29 us
    pallas_call x1, Pallas kernels: 94.9 us -> 84.7 us  [on_device(): pl.pallas_call(functools.partial(encoder_kernel, sections, groups, toks),...]
    unnamed x3 -> x0, local copies, waits for them, and re-layouts: 4.32 us -> none
    pallas_call x0 -> x1, Pallas kernels: none -> 1.07 us  [on_device(): pl.pallas_call(functools.partial(finish_kernel, groups), out_shape=(jax.S...]
where the time goes in v2:
time: 87.3 us; the launch traced here: 87.1 us
  Pallas kernels  85.8 us (98%)
  between operations  1.29 us (1%)
    pallas_call x1, Pallas kernels, on_device(): pl.pallas_call(functools.partial(encoder_kernel, sections, groups, toks),...  84.7 us

profile of v2, /device:TPU:0, one launch (start us, length us, event | category | flops | bytes accessed | tf_op | source)
XLA Modules:
  0.0 87.1 jit_solution(2430648098798275970)
XLA Ops:
  1.3 84.7 %shard_map.156 = (bf16[8,8,256]{2,1,0:T(8,128)(2,1)S(1)}, f32[8,1,128]{2,1,0:T(1,128)S(1)}, bf16[1024,64]{1,0:T(8,128)(2,1)S(1)}, bf16[1024,256]{1,0:T(8,128)(2,1)S(1)}) custom-call(bf16[197,8,1024]{2,1,0:T(8,128)(2,1)} %bitcast.5, bf16[8,256]{1,0:T(8,128)(2,1)} %online_hbm.1, f32[1,1024]{1,0:T(1,128)} %gain_one_hbm.1, f32[1,1024]{1,0:T(1,128)} %gain_two_hbm.1, ...), custom_call_target="tpu_custom_call" | custom-call | flops 26440892416 | bytes 16777216 | tf_op jit(solution)/shard_map/pallas_call | solution.py:594
  86.0 1.1 %shard_map.157 = (bf16[8,256]{1,0:T(8,128)(2,1)}, f32[1,8]{1,0:T(1,128)}, f32[1,1]{1,0:T(1,128)}, bf16[1024,256]{1,0:T(8,128)(2,1)}) custom-call(bf16[8,8,256]{2,1,0:T(8,128)(2,1)S(1)} %get-tuple-element.12.all_keys, f32[8,1,128]{2,1,0:T(1,128)S(1)} %get-tuple-element.13.losses, bf16[1024,64]{1,0:T(8,128)(2,1)S(1)} %get-tuple-element.14.place, ...), custom_call_target="tpu_custom_call" | custom-call | tf_op jit(solution)/shard_map/pallas_call | solution.py:672
